TPU v7x, 32 devices: a whole 2x2x4 slice. The times are simulated.
32 devices in a mesh: groups: 2 (over y), rows: 4 (over z), cols: 2 (over x), sub: 2 (over core).
Axes of the slice: x: 2, y: 2, z: 4, core: 2. Of those that a mesh axis runs over, the one named last changes fastest.
Arguments:
- stored_vectors: bfloat16 [3072, 8192], P(('cols', 'sub'), ('groups', 'rows')), parts along dimension 1, may hold values from -0.59765625 to 0.59765625
- previous_columns: bfloat16 [8192, 256], P(('groups', 'rows', 'cols', 'sub')), parts along dimension 0, may hold values from -3 to 3
- pivots: int32 [512], P('groups'), parts along dimension 0, may hold values from 0 to 4095, as said below
- diagonal: float32 [8192], P(('groups', 'rows', 'cols', 'sub')), parts along dimension 0, may hold values from 2 to 32
- ket_blocks: bfloat16 [128, 128, 256], P(('groups', 'rows', 'cols', 'sub')), parts along dimension 0, may hold values from -6 to 6
- shell_tags: int32 [128, 128], P(('groups', 'rows', 'cols', 'sub')), parts along dimension 0, may hold values from 0 to 3
- target_blocks: int32 [32, 4], P('groups'), parts along dimension 0, may hold values from 0 to 31, as said below
- block_counts: int32 [32], P('groups'), parts along dimension 0, may hold values from 0 to 4, as said below
- shell_norms: float32 [4], replicated, may hold values from 0.5 to 2
Outputs:
- new_vectors: bfloat16 [8192, 256], P(('groups', 'rows', 'cols', 'sub')), parts along dimension 0
- diag_out: float32 [8192], P(('groups', 'rows', 'cols', 'sub')), parts along dimension 0
- next_columns: bfloat16 [8192, 256], P(('groups', 'rows', 'cols', 'sub')), parts along dimension 0
There are 2 independent parts, one for each index of `groups`. A program takes and returns all parts, laid end to end along the dimension named above; an argument that names none is the same for every part. Nothing has to cross between parts.
Inputs may be any that keep to these rules, and one draw needn't show every extreme that they name: `pivots`: 256 distinct AO pairs. `target_blocks`: the used slots of all owners name every block of the 32 blocks exactly once; a used slot's block lies on a device with the owner's cols and sub indices (blocks g * 2 to g * 2 + 1 lie on the device of linear index g, rows slowest; owner o is the device of linear index o). At most 1 of one owner's used slots go to one device, and some owner reaches that in every draw. Entries of unused slots are arbitrary blocks. `block_counts`: some owner uses all 4 slots in every draw.
All inputs are finite; a program needn't handle non-finite values.
Results may differ from a plain program's by a relative error of at most 0.0004.
Values may be sent and summed in bfloat16 or wider, within the bound.
No kernel may reach another device: no remote copies, remote signals or barrier semaphores. Data moves between devices by JAX's collectives and lax.ppermute only.
A program may use at most 64 MiB of HBM per device.

v0:
```python
import jax
import jax.numpy as jnp
from jax import lax
from jax.sharding import PartitionSpec as P


def slot_plan(row_targets, count, column_size, per_device):
    slot_count = row_targets.shape[0]
    slots = jnp.arange(slot_count, dtype=jnp.int32)
    valid = slots < count
    receiver = row_targets // (column_size * per_device)
    within = row_targets % per_device
    earlier = (
        (receiver[:, None] == receiver[None, :])
        & valid[:, None]
        & valid[None, :]
        & (slots[None, :] < slots[:, None])
    )
    ranking = jnp.sum(earlier.astype(jnp.int32), axis=1)
    return (valid, receiver, ranking, within)


def body(
    stored_vectors,
    previous_columns,
    pivots,
    diagonal,
    ket_blocks,
    shell_tags,
    target_blocks,
    block_counts,
    shell_norms,
):
    rows_here = previous_columns.shape[0]
    batch = previous_columns.shape[1]
    block_rows = ket_blocks.shape[1]
    slot_count = ket_blocks.shape[0]
    per_device = rows_here // block_rows
    band_rows = stored_vectors.shape[1]
    band_index = lax.axis_index("rows")
    device_index = lax.axis_index(("rows", "cols", "sub"))
    column_index = lax.axis_index(("cols", "sub"))
    column_size = lax.axis_size(("cols", "sub"))
    band_size = lax.axis_size("rows")
    peer_slots = (slot_count + band_size - 1) // band_size
    local_pivots = pivots - device_index * rows_here
    matches = jnp.arange(rows_here, dtype=jnp.int32)[:, None] == local_pivots[None, :]
    diag_terms = jnp.sum(jnp.where(matches, diagonal[:, None], jnp.float32(0.0)), axis=0)
    pivot_diag = lax.psum(diag_terms, ("rows", "cols", "sub"))
    band_pivots = pivots - band_index * band_rows
    inside = (band_pivots >= 0) & (band_pivots < band_rows)
    clamped = jnp.clip(band_pivots, 0, band_rows - 1)
    taken = jnp.take(stored_vectors, clamped, axis=1).astype(jnp.float32)
    picked = jnp.where(inside[None, :], taken, jnp.float32(0.0))
    pivot_rows = lax.psum(picked, "rows").astype(jnp.bfloat16)
    kinds = jnp.arange(shell_norms.shape[0], dtype=jnp.int32)
    factor = jnp.sum(
        jnp.where(shell_tags[..., None] == kinds, shell_norms, jnp.float32(0.0)), axis=-1
    )
    fresh = (ket_blocks.astype(jnp.float32) * factor[..., None]).astype(jnp.bfloat16)
    own_targets = lax.dynamic_index_in_dim(target_blocks, device_index, 0, keepdims=False)
    own_count = lax.dynamic_index_in_dim(block_counts, device_index, 0, keepdims=False)
    valid, receiver, ranking, within = slot_plan(own_targets, own_count, column_size, per_device)
    lines = jnp.arange(band_size * peer_slots, dtype=jnp.int32)[:, None]
    routing = (
        (lines // peer_slots == receiver[None, :])
        & (lines % peer_slots == ranking[None, :])
        & valid[None, :]
    ).astype(jnp.bfloat16)
    outgoing = jnp.dot(
        routing, fresh.reshape(slot_count, block_rows * batch), preferred_element_type=jnp.float32
    )
    outgoing = outgoing.astype(jnp.bfloat16).reshape(band_size, peer_slots, block_rows, batch)
    incoming = lax.all_to_all(outgoing, "rows", split_axis=0, concat_axis=0, tiled=True)
    sources = jnp.arange(band_size, dtype=jnp.int32) * column_size + column_index
    source_targets = jnp.take(target_blocks, sources, axis=0)
    source_counts = jnp.take(block_counts, sources, axis=0)
    plan_each = jax.vmap(
        lambda row_targets, count: slot_plan(row_targets, count, column_size, per_device)
    )
    source_valid, source_receiver, source_rank, source_within = plan_each(
        source_targets, source_counts
    )
    arriving = source_valid & (source_receiver == band_index)
    places = jnp.arange(per_device, dtype=jnp.int32)[:, None, None, None]
    peer_lines = jnp.arange(peer_slots, dtype=jnp.int32)[None, None, :, None]
    hits = (
        (source_within[None, :, None, :] == places)
        & (source_rank[None, :, None, :] == peer_lines)
        & arriving[None, :, None, :]
    )
    placement = (
        jnp.any(hits, axis=3).astype(jnp.bfloat16).reshape(per_device, band_size * peer_slots)
    )
    arranged = jnp.dot(
        placement,
        incoming.reshape(band_size * peer_slots, block_rows * batch),
        preferred_element_type=jnp.float32,
    )
    next_columns = arranged.astype(jnp.bfloat16).reshape(rows_here, batch)
    product = lax.psum_scatter(
        lax.dot_general(
            stored_vectors, pivot_rows, (((0,), (0,)), ((), ())), preferred_element_type=jnp.float32
        ),
        ("cols", "sub"),
        scatter_dimension=0,
        tiled=True,
    )
    residual_cols = previous_columns.astype(jnp.float32) - product
    scaled = residual_cols / jnp.sqrt(pivot_diag)[None, :]
    new_vectors = scaled.astype(jnp.bfloat16)
    diag_out = diagonal - jnp.sum(scaled * scaled, axis=1)
    return (new_vectors, diag_out, next_columns)


def solution(mesh):
    return jax.shard_map(
        body,
        mesh=mesh,
        in_specs=(
            P(("cols", "sub"), ("groups", "rows")),
            P(("groups", "rows", "cols", "sub"), None),
            P("groups"),
            P(("groups", "rows", "cols", "sub")),
            P(("groups", "rows", "cols", "sub"), None, None),
            P(("groups", "rows", "cols", "sub"), None),
            P("groups", None),
            P("groups"),
            P(),
        ),
        out_specs=(
            P(("groups", "rows", "cols", "sub"), None),
            P(("groups", "rows", "cols", "sub")),
            P(("groups", "rows", "cols", "sub"), None),
        ),
        check_vma=False,
    )
```

profile of v0, /device:TPU:0, one launch (start us, length us, event | category | flops | bytes accessed | tf_op | source)
XLA Modules:
  0.0 100.1 jit_solution(16816415105481037228)
XLA Ops:
  7.2 1.7 %copy.26 = bf16[768,1024]{0,1:T(8,128)(2,1)S(1)} copy(bf16[768,1024]{1,0:T(8,128)(2,1)} %param.9) | data formatting | bytes 3145728 | tf_op args[0]
  9.0 1.2 %gather_fusion = bf16[256,768]{1,0:T(8,128)(2,1)S(1)} fusion(bf16[768,1024]{0,1:T(8,128)(2,1)S(1)} %copy.26, s32[1024]{0:T(1024)S(1)} %pad_clamp_fusion.1), kind=kCustom, calls=%fused_computation | custom fusion | bytes 787456 | tf_op jit(solution)/shard_map/jit(_take)/gather | solution.py:53
  10.2 0.2 select_bitcast_fusion
  10.4 37.4 %all-reduce.1 = bf16[768,256]{0,1:T(8,128)(2,1)S(1)} all-reduce(f32[768,256]{0,1:T(8,128)S(1)} %select_bitcast_fusion), channel_id=1, replica_groups=mesh['groups'=2,'rows'=4,'cols'=2,'sub'=2] {'rows'}, use_global_device_ids=true, to_apply=%region_0.1 | all-reduce | flops 196608 | bytes 1179648 | tf_op jit(solution)/shard_map/psum | solution.py:55
  47.9 1.6 %convolution_bitcast_fusion = f32[1024,256]{0,1:T(8,128)} fusion(bf16[768,1024]{1,0:T(8,128)(2,1)S(1)} %copy-done.1, bf16[768,256]{0,1:T(8,128)(2,1)S(1)} %all-reduce.1), kind=kOutput, calls=%fused_computation.5 | convolution fusion | flops 402653184 | bytes 3014656 | tf_op jit(solution)/shard_map/dot_general | solution.py:102
  49.7 0.2 copy.30
  50.0 0.2 copy-done.4
  50.1 0.2 dynamic-slice_reduce_fusion
  50.3 0.6 dynamic_slice.9
  50.9 0.6 iota_compare_fusion.6
  51.6 0.2 convert_reduce_fusion.1
  51.8 0.3 convolution_convert_fusion
  52.1 0.7 copy.34
  52.8 3.4 %all-to-all-start = ((bf16[4,1,128,256]{3,2,1,0:T(8,128)(2,1)}), bf16[4,1,128,256]{3,2,1,0:T(8,128)(2,1)S(1)}, u32[]{:S(2)}, u32[]{:S(2)}) async-start(bf16[4,1,128,256]{3,2,1,0:T(8,128)(2,1)} %bitcast.26), calls=%async_computation.1 | async-start | bytes 524288 | tf_op jit(solution)/shard_map/all_to_all | solution.py:74
  56.3 0.6 gather_fusion.2
  57.0 0.6 gather_fusion.1
  57.6 0.2 convert_reduce_fusion
  58.0 31.2 %psum.15 = f32[256]{0:T(256)S(1)} all-reduce(f32[256]{0:T(256)S(1)} %select_reduce_fusion), channel_id=1, replica_groups=mesh['groups'=2,'rows'=4,'cols'=2,'sub'=2] {'rows','cols','sub'}, use_global_device_ids=true, to_apply=%region_3.4 | all-reduce | flops 256 | bytes 2048 | tf_op jit(solution)/shard_map/psum | solution.py:49
  89.6 0.2 copy.32
  89.8 0.3 convolution_convert_fusion.1
  90.1 0.7 reshape.328
  90.8 1.1 %multiply_reduce_fusion = (f32[256]{0:T(256)S(1)}, bf16[256,256]{0,1:T(8,128)(2,1)S(1)}) fusion(f32[256]{0:T(256)S(1)} %sqrt.3, f32[256,256]{0,1:T(8,128)} %reduce-scatter.2.cloned.1.call-done, bf16[256,256]{0,1:T(8,128)(2,1)S(1)} %copy.25), kind=kLoop, calls=%fused_computation.11 | loop fusion | flops 392960 | bytes 526336 | tf_op jit(solution)/shard_map/reduce_sum | solution.py:112
  91.9 0.8 copy.29
  92.6 0.6 sub.35
  (40 shorter events, 1.0 us)
Async XLA Ops:
  7.2 83.6 %reduce-scatter.2.cloned.1.call-start = ((), (), s32[]{:S(2)}) async-start(), calls=%async_computation.2 | async-start | bytes 1310720 | tf_op jit(solution)/shard_map/reduce_scatter | solution.py:101
  7.2 1.7 %copy-start.6 = (s32[256]{0:T(256)S(1)}, s32[256]{0:T(256)}, u32[]{:S(2)}) copy-start(s32[256]{0:T(256)} %param.11) | copy-start | bytes 3076
  10.2 37.6 %copy-start.1 = (bf16[768,1024]{1,0:T(8,128)(2,1)S(1)}, bf16[768,1024]{1,0:T(8,128)(2,1)}, u32[]{:S(2)}) copy-start(bf16[768,1024]{1,0:T(8,128)(2,1)} %param.9) | copy-start | bytes 4718596
  47.8 1.6 %copy-start.7 = (s32[4,128]{1,0:T(4,128)S(1)}, s32[4,128]{1,0:T(4,128)}, u32[]{:S(2)}) copy-start(s32[4,128]{1,0:T(4,128)} %param.14) | copy-start | bytes 6148
  47.8 1.6 %copy-start.8 = (f32[4]{0:T(128)S(1)}, f32[4]{0:T(128)}, u32[]{:S(2)}) copy-start(f32[4]{0:T(128)} %param.17) | copy-start | bytes 52
  47.9 1.7 %copy-start.2 = (bf16[4,128,256]{2,1,0:T(8,128)(2,1)S(1)}, bf16[4,128,256]{2,1,0:T(8,128)(2,1)}, u32[]{:S(2)}) copy-start(bf16[4,128,256]{2,1,0:T(8,128)(2,1)} %param.13) | copy-start | bytes 786436
  49.4 0.7 copy-start.4
  49.4 0.9 copy-start
  49.6 8.3 %copy-start.5 = (f32[256]{0:T(256)S(1)}, f32[256]{0:T(256)}, u32[]{:S(2)}) copy-start(f32[256]{0:T(256)} %param.12) | copy-start | bytes 3076
  49.6 39.6 %copy-start.3 = (bf16[256,256]{1,0:T(8,128)(2,1)S(1)}, bf16[256,256]{1,0:T(8,128)(2,1)}, u32[]{:S(2)}) copy-start(bf16[256,256]{1,0:T(8,128)(2,1)} %param.10) | copy-start | bytes 393220
  52.8 36.7 %all-to-all-start = ((bf16[4,1,128,256]{3,2,1,0:T(8,128)(2,1)}), bf16[4,1,128,256]{3,2,1,0:T(8,128)(2,1)S(1)}, u32[]{:S(2)}, u32[]{:S(2)}) async-start(bf16[4,1,128,256]{3,2,1,0:T(8,128)(2,1)} %bitcast.26), calls=%async_computation.1 | async-start | bytes 524288 | tf_op jit(solution)/shard_map/all_to_all | solution.py:74
Sparse Core Ops, SparseCore 0:
  49.6 24.2 reduce-scatter.1
where the time goes:
time: 100 us
  blocking collectives  68.6 us (69%)
  between operations  14.3 us (14%)
  local copies, waits for them, and re-layouts  7.74 us (8%)
  other arithmetic  3.79 us (4%)
  starting transfers between devices  3.44 us (3%)
  matrix products  2.14 us (2%)
    psum x1, blocking collectives, body(): pivot_rows = lax.psum(picked, 'rows').astype(jnp.bfloat16)  37.4 us
    psum x1, blocking collectives, body(): pivot_diag = lax.psum(diag_terms, ('rows', 'cols', 'sub'))  31.2 us
    unnamed x25, local copies, waits for them, and re-layouts  4.02 us
    all_to_all x1, starting transfers between devices, body(): lax.all_to_all(outgoing, 'rows', split_axis=0, concat_axis=0, tiled=True)  3.4 us
  transfers between devices with their start and end apart: 2, of which 0 were waited for; matrix products, arithmetic and copies ran while one was open for 6% of the time, Pallas kernels for 0%

commit v1 on v0

v1 whole, which is shorter than its diff:
```python
import functools
import math
import jax
import jax.numpy as jnp
from jax import lax
from jax.experimental import pallas as pl
from jax.experimental.pallas import tpu as pltpu
from jax.sharding import PartitionSpec as P

F32 = jnp.float32
BF16 = jnp.bfloat16
I32 = jnp.int32
LANES = 128
SPARE = 3
VMEM = pl.BlockSpec(memory_space=pltpu.VMEM)
SMEM = pl.BlockSpec(memory_space=pltpu.SMEM)


def slots_of(batch, bands):
    mean = batch / bands
    return min(
        -(-(batch + SPARE) // 16) * 16,
        -(-int(mean + 3.6 * math.sqrt(mean) + SPARE) // 16) * 16,
    )


def nt(a, b):
    return lax.dot_general(a, b, (((1,), (1,)), ((), ())), preferred_element_type=F32)


def tn(a, b):
    return lax.dot_general(a, b, (((0,), (0,)), ((), ())), preferred_element_type=F32)


def split3(x):
    high = x.astype(BF16)
    rest = x - high.astype(F32)
    mid = rest.astype(BF16)
    low = (rest - mid.astype(F32)).astype(BF16)
    return high, mid, low


def ranks_in(mask):
    batch = mask.shape[1]
    above = lax.broadcasted_iota(I32, (batch, batch), 0) < lax.broadcasted_iota(
        I32, (batch, batch), 1
    )
    return jnp.dot(mask.astype(BF16), above.astype(BF16), preferred_element_type=F32)


def select_kernel(place_ref, pivots_ref, diag_ref, vectors_ref, out_ref, *, slots):
    cap = slots - SPARE
    width, band_rows = vectors_ref.shape
    batch = pivots_ref.shape[1]
    rows_here = diag_ref.shape[1]
    padded = -(-slots // LANES) * LANES
    band = place_ref[0]
    column = place_ref[1]
    local = pivots_ref[...] - band * band_rows
    mine = (local >= 0) & (local < band_rows)
    rank = ranks_in(jnp.broadcast_to(jnp.where(mine, 1.0, 0.0), (8, batch)))[0:1]
    rank = rank.astype(I32) - place_ref[4]
    line = lax.broadcasted_iota(I32, (padded, batch), 0)
    hit = (rank == line) & mine & (line < cap)
    where = jnp.sum(jnp.where(hit, (local + 1).astype(F32), 0.0), axis=1, keepdims=True)
    where = where.astype(I32) - 1
    chosen = where[:slots] == lax.broadcasted_iota(I32, (slots, band_rows), 1)
    picked = nt(jnp.where(chosen, 1.0, 0.0).astype(BF16), vectors_ref[...])
    out_ref[...] = picked.astype(BF16)
    own = where == column * rows_here + lax.broadcasted_iota(I32, (padded, rows_here), 1)
    high, mid, low = split3(diag_ref[...])
    row = lax.broadcasted_iota(I32, (16, rows_here), 0)
    diag = jnp.where(
        row == 13,
        high.astype(F32),
        jnp.where(row == 14, mid.astype(F32), jnp.where(row == 15, low.astype(F32), 0.0)),
    ).astype(BF16)
    spare = nt(diag, jnp.where(own, 1.0, 0.0).astype(BF16))
    out_ref[slots - 16 :, 0:padded] = (picked[slots - 16 :, 0:padded] + spare).astype(BF16)


def multiply_kernel(place_ref, *refs, pieces, slots, cols, sub, rows_here):
    piece_refs, vectors_ref, keep_ref, send_ref = (
        refs[:pieces],
        refs[pieces],
        refs[pieces + 1],
        refs[pieces + 2],
    )
    padded = -(-slots // LANES) * LANES
    mine_c = place_ref[2]
    mine_s = place_ref[3]
    left = jnp.concatenate([ref[...] for ref in piece_refs], axis=0)
    row = lax.broadcasted_iota(I32, (8, padded), 0)
    for out_ref, way in ((keep_ref, 0), (send_ref, 1)):
        for step in range(cols):
            block = (mine_c ^ step) * sub + (mine_s ^ way)
            start = pl.multiple_of(block * rows_here, LANES)
            got = jnp.dot(
                left, vectors_ref[:, pl.ds(start, rows_here)], preferred_element_type=F32
            )
            at = step * rows_here
            out_ref[:, at : at + rows_here] = got
            for piece in range(pieces):
                low = (piece + 1) * slots - 8
                spare = left[low - 8 : low + 8, 0:padded].astype(F32)[8:16]
                out_ref[low : low + 8, at : at + padded] = jnp.where(
                    row >= 8 - SPARE, spare, got[low : low + 8, 0:padded]
                )


def gather_terms(place_ref, pivots_ref, refs, groups, slots, bands, band_rows, rows_here, offset):
    batch = pivots_ref.shape[1]
    cap = slots - SPARE
    padded = -(-slots // LANES) * LANES
    band = place_ref[0]
    pivots = pivots_ref[...]
    lines = -(-bands // 8) * 8
    number = lax.broadcasted_iota(I32, (lines, batch), 0)
    inside = (pivots >= number * band_rows) & (pivots < (number + 1) * band_rows)
    inside = jnp.where(inside, 1.0, 0.0)
    ranks = ranks_in(inside)
    rank = jnp.sum(inside * ranks, axis=0, keepdims=True).astype(I32) - offset
    home = jnp.sum(inside * number.astype(F32), axis=0, keepdims=True).astype(I32)
    line = lax.broadcasted_iota(I32, (padded, batch), 0)
    product = jnp.zeros((rows_here, batch), F32)
    spare = jnp.zeros((8, batch), F32)
    used = 0
    for sources, count in groups:
        total = refs[used][:, 0:rows_here]
        for ref in refs[used + 1 : used + count]:
            total = total + ref[:, 0:rows_here]
        used += count
        for piece, step in enumerate(sources):
            part = total[piece * slots : (piece + 1) * slots]
            spot = jnp.where(home == (band ^ step), rank, -1)
            place = jnp.where((line == spot) & (line < cap), 1.0, 0.0).astype(BF16)
            for term in split3(part):
                product = product + tn(term, place[:slots])
            spare = spare + jnp.dot(
                part[slots - 8 :, 0:padded].astype(BF16), place, preferred_element_type=F32
            )
    return product, spare


def add_kernel(place_ref, pivots_ref, product_ref, spare_ref, *refs, **sizes):
    product, spare = gather_terms(
        place_ref,
        pivots_ref,
        refs[:-2],
        rows_here=product_ref.shape[0],
        offset=place_ref[4],
        **sizes,
    )
    refs[-2][...] = product_ref[...] + product
    refs[-1][...] = spare_ref[...] + spare


def finish_kernel(place_ref, pivots_ref, diag_ref, previous_ref, *refs, extra, **sizes):
    new_ref, diag_out_ref = refs[-2:]
    rows_here = diag_ref.shape[1]
    product, spare = gather_terms(
        place_ref, pivots_ref, refs[extra:-2], rows_here=rows_here, offset=0, **sizes
    )
    if extra:
        product = product + refs[0][...]
        spare = spare + refs[1][...]
    pivot_diag = jnp.sum(spare[8 - SPARE :], axis=0, keepdims=True)
    scaled = (previous_ref[...].astype(F32) - product) * (1.0 / jnp.sqrt(pivot_diag))
    new_ref[...] = scaled.astype(BF16)
    sums = jnp.sum(scaled * scaled, axis=1, keepdims=True)
    same = lax.broadcasted_iota(I32, (rows_here, rows_here), 0) == lax.broadcasted_iota(
        I32, (rows_here, rows_here), 1
    )
    turned = jnp.sum(jnp.where(same, sums, 0.0), axis=0, keepdims=True)
    diag_out_ref[...] = diag_ref[...] - turned


def ket_kernel(place_ref, norms_ref, targets_ref, counts_ref, tags_ref, ket_ref, out_ref, *, per_device, column_size):
    me = place_ref[0] * column_size + place_ref[1]
    tags = tags_ref[...]
    slot_count = tags.shape[0]
    factor = jnp.zeros(tags.shape, F32)
    for kind in range(norms_ref.shape[0]):
        factor = jnp.where(tags == kind, norms_ref[kind], factor)
    fill = -(-slot_count // 8) * 8 - slot_count
    if fill:
        factor = jnp.concatenate([factor, jnp.zeros((fill, tags.shape[1]), F32)], axis=0)
    factor = factor.T
    for slot in range(slot_count):
        fresh = (ket_ref[slot].astype(F32) * factor[:, slot : slot + 1]).astype(BF16)
        receiver = targets_ref[me, slot] // (column_size * per_device)

        @pl.when(slot < counts_ref[me])
        def _():
            out_ref[receiver] = fresh


def place_kernel(place_ref, targets_ref, counts_ref, incoming_ref, out_ref, *, per_device, column_size):
    me = place_ref[0] * column_size + place_ref[1]
    block_rows = incoming_ref.shape[1]
    for source in range(incoming_ref.shape[0]):
        owner = source * column_size + place_ref[1]
        for slot in range(targets_ref.shape[1]):
            block = targets_ref[owner, slot]

            @pl.when((slot < counts_ref[owner]) & (block // per_device == me))
            def _():
                start = pl.multiple_of((block % per_device) * block_rows, block_rows)
                out_ref[pl.ds(start, block_rows), :] = incoming_ref[source]


def call(kernel, outs, specs, args, name):
    return pl.pallas_call(
        kernel,
        out_shape=outs,
        in_specs=specs,
        out_specs=jax.tree.map(lambda _: VMEM, outs),
        name=name,
    )(*args)


def body(
    stored_vectors,
    previous_columns,
    pivots,
    diagonal,
    ket_blocks,
    shell_tags,
    target_blocks,
    block_counts,
    shell_norms,
    *,
    bands,
    cols,
    sub,
):
    rows_here, batch = previous_columns.shape
    width, band_rows = stored_vectors.shape
    block_rows = ket_blocks.shape[1]
    per_device = rows_here // block_rows
    slots = slots_of(batch, bands)
    cap = slots - SPARE
    band_index = lax.axis_index("rows")
    cols_index = lax.axis_index("cols")
    sub_index = lax.axis_index("sub")
    place = jnp.stack(
        [band_index, cols_index * sub + sub_index, cols_index, sub_index, jnp.int32(0)]
    ).astype(I32)
    pivot_line = pivots.reshape(1, batch)
    diag_line = diagonal.reshape(1, rows_here)

    def swap(x, axis, size, step):
        return lax.ppermute(x, axis, [(i, i ^ step) for i in range(size)])

    def select(where):
        return call(
            functools.partial(select_kernel, slots=slots),
            jax.ShapeDtypeStruct((slots, width), BF16),
            [SMEM, VMEM, VMEM, VMEM],
            (where, pivot_line, diag_line, stored_vectors),
            "select",
        )

    def reduce_group(pieces):
        count = len(pieces)
        out = jax.ShapeDtypeStruct((count * slots, cols * rows_here), F32)
        keep, send = call(
            functools.partial(
                multiply_kernel,
                pieces=count,
                slots=slots,
                cols=cols,
                sub=sub,
                rows_here=rows_here,
            ),
            (out, out),
            [SMEM] + [VMEM] * (count + 1),
            (place, *pieces, stored_vectors),
            "multiply",
        )
        terms = [keep, swap(send, "sub", sub, 1)]
        step = cols // 2
        while step:
            at = step * rows_here
            upper = terms[0][:, at : 2 * at]
            for term in terms[1:]:
                upper = upper + term[:, at : 2 * at]
            terms.append(swap(upper, "cols", cols, step))
            step //= 2
        return terms

    def settings(groups):
        meta = tuple((sources, len(terms)) for sources, terms in groups)
        arrays = [term for _, terms in groups for term in terms]
        return dict(groups=meta, slots=slots, bands=bands, band_rows=band_rows), arrays

    def finish(groups, before=()):
        sizes, arrays = settings(groups)
        arrays = [*before, *arrays]
        return call(
            functools.partial(finish_kernel, extra=len(before), **sizes),
            (
                jax.ShapeDtypeStruct((rows_here, batch), BF16),
                jax.ShapeDtypeStruct((1, rows_here), F32),
            ),
            [SMEM] + [VMEM] * (3 + len(arrays)),
            (place, pivot_line, diag_line, previous_columns, *arrays),
            "finish",
        )

    def gather(own):
        order = sorted(range(1, bands), key=lambda d: (d != bands - 1, d))
        return {0: own, **{d: swap(own, "rows", bands, d) for d in order}}

    held = gather(select(place))
    rest = tuple(range(2, bands))
    main = [(0,), (1,)][:bands] + ([rest] if rest else [])
    groups = [(s, reduce_group([held[d] for d in s])) for s in main]

    outgoing = call(
        functools.partial(ket_kernel, per_device=per_device, column_size=cols * sub),
        jax.ShapeDtypeStruct((bands,) + ket_blocks.shape[1:], BF16),
        [SMEM, SMEM, SMEM, SMEM, VMEM, VMEM],
        (place, shell_norms, target_blocks, block_counts, shell_tags, ket_blocks),
        "ket",
    )
    if bands > 1:
        outgoing, _ = lax.optimization_barrier((outgoing, held[bands - 1]))
    incoming = lax.all_to_all(outgoing, "rows", split_axis=0, concat_axis=0, tiled=True)
    next_columns = call(
        functools.partial(place_kernel, per_device=per_device, column_size=cols * sub),
        jax.ShapeDtypeStruct((rows_here, batch), BF16),
        [SMEM, SMEM, SMEM, VMEM],
        (place, target_blocks, block_counts, incoming),
        "place",
    )

    def plain():
        return finish(groups)

    def further():
        every = tuple(range(bands))

        def step(number, sums):
            where = place.at[4].set(number * cap)
            pieces = gather(select(where))
            sizes, arrays = settings([(every, reduce_group([pieces[d] for d in every]))])
            return call(
                functools.partial(add_kernel, **sizes),
                tuple(jax.ShapeDtypeStruct(x.shape, F32) for x in sums),
                [SMEM] + [VMEM] * (3 + len(arrays)),
                (where, pivot_line, *sums, *arrays),
                "add",
            )

        start = (jnp.zeros((rows_here, batch), F32), jnp.zeros((8, batch), F32))
        return finish(groups, lax.fori_loop(1, -(-batch // cap), step, start))

    if cap < batch:
        homes = pivots // band_rows
        held_by = jnp.sum(
            (homes[None, :] == jnp.arange(bands, dtype=I32)[:, None]).astype(I32), axis=1
        )
        new_vectors, diag_out = lax.cond(jnp.max(held_by) > cap, further, plain)
    else:
        new_vectors, diag_out = plain()
    return (new_vectors, diag_out.reshape(rows_here), next_columns)


def solution(mesh):
    sizes = dict(mesh.shape)
    return jax.shard_map(
        functools.partial(body, bands=sizes["rows"], cols=sizes["cols"], sub=sizes["sub"]),
        mesh=mesh,
        in_specs=(
            P(("cols", "sub"), ("groups", "rows")),
            P(("groups", "rows", "cols", "sub"), None),
            P("groups"),
            P(("groups", "rows", "cols", "sub")),
            P(("groups", "rows", "cols", "sub"), None, None),
            P(("groups", "rows", "cols", "sub"), None),
            P("groups", None),
            P("groups"),
            P(),
        ),
        out_specs=(
            P(("groups", "rows", "cols", "sub"), None),
            P(("groups", "rows", "cols", "sub")),
            P(("groups", "rows", "cols", "sub"), None),
        ),
        check_vma=False,
    )
```

time: 100 us -> 46.2 us (0.46)
  blocking collectives: 68.6 us -> 0 us
  Pallas kernels: 0 us -> 15.8 us
  between operations: 14.3 us -> 1.36 us
  starting transfers between devices: 3.44 us -> 13.4 us
  waiting for transfers between devices: 0.02 us -> 8.46 us
  local copies, waits for them, and re-layouts: 7.74 us -> 2.81 us
  matrix products: 2.14 us -> 0 us
    psum x2 -> x0, blocking collectives: 68.6 us -> none  [the longest x1 37.4 us: body(): pivot_rows = lax.psum(picked, 'rows').astype(jnp.bfloat16)]
    pallas_call x0 -> x7, Pallas kernels: none -> 15.8 us  [call(): pl.pallas_call(kernel, out_shape=outs, in_specs=specs, out_specs=jax.tree...]
    ppermute x0 -> x9, starting transfers between devices: none -> 9.67 us  [swap(): return lax.ppermute(x, axis, [(i, i ^ step) for i in range(size)])]
    ppermute x0 -> x9, waiting for transfers between devices: none -> 7.52 us  [swap(): return lax.ppermute(x, axis, [(i, i ^ step) for i in range(size)])]
    gather x3 -> x0, local copies, waits for them, and re-layouts: 2.39 us -> none  [the longest x1 1.19 us: body(): taken = jnp.take(stored_vectors, clamped, axis=1).astype(jnp.float32)]
    dot_general x3 -> x0, matrix products: 2.14 us -> none  [the longest x1 1.57 us: body(): lax.dot_general(stored_vectors, pivot_rows, (((0,), (0,)), ((), ())), pre...]
    add x0 -> x3, other arithmetic: none -> 2.04 us  [reduce_group(): upper = upper + term[:, at:2 * at]]
    reduce_max x0 -> x1, other arithmetic: none -> 1.29 us  [body(): new_vectors, diag_out = lax.cond(jnp.max(held_by) > cap, further, plain)]
  transfers between devices with their start and end apart: 2 -> 10, of which waited for: 0 -> 3; matrix products, arithmetic and copies ran while one was open for 6% -> 10% of each run, Pallas kernels for 0% -> 22%
where the time goes in v1:
time: 46.2 us; the launch traced here: 45.9 us
  Pallas kernels  15.8 us (34%)
  starting transfers between devices  13.4 us (29%)
  waiting for transfers between devices  8.46 us (18%)
  other arithmetic  3.97 us (9%)
  local copies, waits for them, and re-layouts  2.81 us (6%)
  between operations  1.36 us (3%)
    pallas_call x7, Pallas kernels, call(): pl.pallas_call(kernel, out_shape=outs, in_specs=specs, out_specs=jax.tree...  15.8 us
    ppermute x9, starting transfers between devices, swap(): return lax.ppermute(x, axis, [(i, i ^ step) for i in range(size)])  9.67 us
    ppermute x9, waiting for transfers between devices, swap(): return lax.ppermute(x, axis, [(i, i ^ step) for i in range(size)])  7.52 us
    all_to_all x1, starting transfers between devices, body(): lax.all_to_all(outgoing, 'rows', split_axis=0, concat_axis=0, tiled=True)  3.77 us
    unnamed x19, local copies, waits for them, and re-layouts  2.73 us
    add x3, other arithmetic, reduce_group(): upper = upper + term[:, at:2 * at]  2.04 us
    reduce_max x1, other arithmetic, body(): new_vectors, diag_out = lax.cond(jnp.max(held_by) > cap, further, plain)  1.29 us
    all_to_all x1, waiting for transfers between devices, body(): lax.all_to_all(outgoing, 'rows', split_axis=0, concat_axis=0, tiled=True)  0.94 us
  transfers between devices with their start and end apart: 10, of which 3 were waited for; matrix products, arithmetic and copies ran while one was open for 10% of the time, Pallas kernels for 22%

profile of v1, /device:TPU:0, one launch (start us, length us, event | category | flops | bytes accessed | tf_op | source)
XLA Modules:
  0.0 45.9 jit_solution(13971822289697113579)
XLA Ops:
  0.7 3.0 %select.15.refs_0_ = bf16[96,768]{1,0:T(8,128)(2,1)} custom-call(s32[5]{0:T(128)S(1)} %stack.19.place_ref, s32[1,256]{1,0:T(1,128)} %bitcast.11, f32[1,256]{1,0:T(1,128)} %bitcast.14, bf16[768,1024]{1,0:T(8,128)(2,1)} %refs_2_.1), custom_call_target="tpu_custom_call" | custom-call | tf_op jit(solution)/shard_map/select/pallas_call | solution.py:213
  3.8 5.1 %collective-permute-start.11 = (bf16[96,768]{1,0:T(8,128)(2,1)}, bf16[96,768]{1,0:T(8,128)(2,1)S(1)}, u32[]{:S(2)}, u32[]{:S(2)}) collective-permute-start(bf16[96,768]{1,0:T(8,128)(2,1)} %select.15.refs_0_), channel_id=1, source_target_pairs={{0,12},{4,8},{8,4},{12,0},{1,13},{5,9},{9,5},{13,1},{2,14},{6,10},... | collective-permute-start | bytes 442376 | tf_op jit(solution)/shard_map/ppermute | solution.py:253
  8.8 0.6 %collective-permute-start.7 = (bf16[96,768]{1,0:T(8,128)(2,1)}, bf16[96,768]{1,0:T(8,128)(2,1)S(1)}, u32[]{:S(2)}, u32[]{:S(2)}) collective-permute-start(bf16[96,768]{1,0:T(8,128)(2,1)} %select.15.refs_0_), channel_id=1, source_target_pairs={{0,4},{4,0},{8,12},{12,8},{1,5},{5,1},{9,13},{13,9},{2,6},{6,2},{1... | collective-permute-start | bytes 442376 | tf_op jit(solution)/shard_map/ppermute | solution.py:253
  9.4 2.0 %multiply.16 = (f32[96,512]{1,0:T(8,128)S(1)}, f32[96,512]{1,0:T(8,128)}) custom-call(s32[5]{0:T(128)S(1)} %stack.19.place_ref, bf16[96,768]{1,0:T(8,128)(2,1)} %select.15.refs_0_, bf16[768,1024]{1,0:T(8,128)(2,1)S(1)} %copy-done), custom_call_target="tpu_custom_call" | custom-call | tf_op jit(solution)/shard_map/multiply/pallas_call | solution.py:213
  11.5 0.7 %copy.15.targets_ref = s32[16,4]{1,0:T(8,128)} copy(s32[16,4]{0,1:T(4,128)S(1)} %copy-done.20) | data formatting | bytes 512 | tf_op args[6]
  12.2 2.1 %ket.1 = bf16[4,128,256]{2,1,0:T(8,128)(2,1)} custom-call(s32[5]{0:T(128)S(1)} %stack.19.place_ref, f32[4]{0:T(128)} %norms_ref.1, s32[16,4]{1,0:T(8,128)} %copy.15.targets_ref, s32[16]{0:T(128)} %counts_ref.3, s32[4,128]{1,0:T(4,128)} %tags_ref.1, bf16[4,128,256]{2,1,0:T(8,128)(2,1)} %ket_ref.1), custom_call_target="tpu_custom_call" | custom-call | tf_op jit(solution)/shard_map/ket/pallas_call | solution.py:213
  14.3 7.3 %collective-permute-done.10.refs_0_ = bf16[96,768]{1,0:T(8,128)(2,1)S(1)} collective-permute-done((bf16[96,768]{1,0:T(8,128)(2,1)}, bf16[96,768]{1,0:T(8,128)(2,1)S(1)}, u32[]{:S(2)}, u32[]{:S(2)}) %collective-permute-start.10) | collective-permute-done | bytes 147488 | tf_op jit(solution)/shard_map/ppermute | solution.py:253
  21.5 0.7 %copy-done.16 = bf16[96,768]{1,0:T(8,128)(2,1)} copy-done((bf16[96,768]{1,0:T(8,128)(2,1)}, bf16[96,768]{1,0:T(8,128)(2,1)S(1)}, u32[]{:S(2)}) %copy-start.16) | copy-done | bytes 147480
  22.2 2.2 %multiply.18 = (f32[192,512]{1,0:T(8,128)S(1)}, f32[192,512]{1,0:T(8,128)}) custom-call(s32[5]{0:T(128)S(1)} %stack.19.place_ref, bf16[96,768]{1,0:T(8,128)(2,1)} %copy-done.16, bf16[96,768]{1,0:T(8,128)(2,1)} %copy-done.15, bf16[768,1024]{1,0:T(8,128)(2,1)S(1)} %copy-done), custom_call_target="tpu_custom_call" | custom-call | tf_op jit(solution)/shard_map/multiply/pallas_call | solution.py:213
  24.5 0.7 %copy-done.14 = bf16[96,768]{1,0:T(8,128)(2,1)} copy-done((bf16[96,768]{1,0:T(8,128)(2,1)}, bf16[96,768]{1,0:T(8,128)(2,1)S(1)}, u32[]{:S(2)}) %copy-start.14) | copy-done | bytes 147480
  25.2 2.0 %multiply.17 = (f32[96,512]{1,0:T(8,128)S(1)}, f32[96,512]{1,0:T(8,128)}) custom-call(s32[5]{0:T(128)S(1)} %stack.19.place_ref, bf16[96,768]{1,0:T(8,128)(2,1)} %copy-done.14, bf16[768,1024]{1,0:T(8,128)(2,1)S(1)} %copy-done), custom_call_target="tpu_custom_call" | custom-call | tf_op jit(solution)/shard_map/multiply/pallas_call | solution.py:213
  27.7 3.8 %all-to-all-start = ((bf16[4,128,256]{2,1,0:T(8,128)(2,1)}), bf16[4,128,256]{2,1,0:T(8,128)(2,1)S(1)}, u32[]{:S(2)}, u32[]{:S(2)}) async-start(bf16[4,128,256]{2,1,0:T(8,128)(2,1)} %ket.1), calls=%async_computation | async-start | bytes 524288 | tf_op jit(solution)/shard_map/all_to_all | solution.py:329
  31.4 0.7 %slice_add_fusion.3 = f32[96,256]{1,0:T(8,128)} fusion(f32[96,512]{1,0:T(8,128)S(1)} %collective-permute-done.5, f32[96,512]{1,0:T(8,128)S(1)} %get-tuple-element.320), kind=kLoop, calls=%fused_computation.4 | loop fusion | flops 24576 | bytes 294912 | tf_op jit(solution)/shard_map/add | solution.py:287
  32.1 1.5 %collective-permute-start.6 = (f32[96,256]{1,0:T(8,128)}, f32[96,256]{1,0:T(8,128)}, u32[]{:S(2)}, u32[]{:S(2)}) collective-permute-start(f32[96,256]{1,0:T(8,128)} %slice_add_fusion.3), channel_id=1, source_target_pairs={{0,2},{2,0},{1,3},{3,1},{4,6},{6,4},{5,7},{7,5},{8,10},{10,8},{9,1... | collective-permute-start | bytes 294920 | tf_op jit(solution)/shard_map/ppermute | solution.py:253
  33.6 0.7 %slice_add_fusion.1 = f32[192,256]{1,0:T(8,128)} fusion(f32[192,512]{1,0:T(8,128)S(1)} %collective-permute-done.12, f32[192,512]{1,0:T(8,128)S(1)} %get-tuple-element.324), kind=kLoop, calls=%fused_computation.2 | loop fusion | flops 49152 | bytes 589824 | tf_op jit(solution)/shard_map/add | solution.py:287
  34.8 0.7 %slice_add_fusion.2 = f32[96,256]{1,0:T(8,128)} fusion(f32[96,512]{1,0:T(8,128)S(1)} %collective-permute-done.8, f32[96,512]{1,0:T(8,128)S(1)} %get-tuple-element.322), kind=kLoop, calls=%fused_computation.3 | loop fusion | flops 24576 | bytes 294912 | tf_op jit(solution)/shard_map/add | solution.py:287
  35.5 1.5 %collective-permute-start.9 = (f32[96,256]{1,0:T(8,128)}, f32[96,256]{1,0:T(8,128)}, u32[]{:S(2)}, u32[]{:S(2)}) collective-permute-start(f32[96,256]{1,0:T(8,128)} %slice_add_fusion.2), channel_id=1, source_target_pairs={{0,2},{2,0},{1,3},{3,1},{4,6},{6,4},{5,7},{7,5},{8,10},{10,8},{9,1... | collective-permute-start | bytes 294920 | tf_op jit(solution)/shard_map/ppermute | solution.py:253
  37.0 0.6 %convert_reduce_fusion = s32[4]{0:T(128)} fusion(s32[256]{0:T(256)S(1)} %and_select_fusion), kind=kLoop, calls=%fused_computation.5 | loop fusion | flops 3068 | bytes 1040 | tf_op jit(solution)/shard_map/reduce_sum | solution.py:361
  37.6 1.3 %reduce_max.9 = s32[]{:T(128)} reduce(s32[4]{0:T(128)} %convert_reduce_fusion, s32[]{:T(128)} %constant.110.clone.1), dimensions={0}, to_apply=%region_1.2 | reduce | flops 3 | bytes 24 | tf_op jit(solution)/shard_map/reduce_max | solution.py:364
  39.6 0.9 %all-to-all-done.incoming_ref = bf16[4,128,256]{2,1,0:T(8,128)(2,1)S(1)} async-done(((bf16[4,128,256]{2,1,0:T(8,128)(2,1)}), bf16[4,128,256]{2,1,0:T(8,128)(2,1)S(1)}, u32[]{:S(2)}, u32[]{:S(2)}) %all-to-all-start) | async-done | bytes 262176 | tf_op jit(solution)/shard_map/all_to_all | solution.py:329
  40.5 0.7 %copy-done.11 = bf16[4,128,256]{2,1,0:T(8,128)(2,1)} copy-done((bf16[4,128,256]{2,1,0:T(8,128)(2,1)}, bf16[4,128,256]{2,1,0:T(8,128)(2,1)S(1)}, u32[]{:S(2)}) %copy-start.11) | copy-done | bytes 262168
  41.2 1.9 %place.1 = bf16[256,256]{1,0:T(8,128)(2,1)} custom-call(s32[5]{0:T(128)S(1)} %stack.19.place_ref, s32[16,4]{1,0:T(8,128)} %copy.15.targets_ref, s32[16]{0:T(128)} %counts_ref.3, bf16[4,128,256]{2,1,0:T(8,128)(2,1)} %copy-done.11), custom_call_target="tpu_custom_call" | custom-call | tf_op jit(solution)/shard_map/place/pallas_call | solution.py:213
  43.4 2.5 %conditional.1 = (bf16[256,256]{1,0:T(8,128)(2,1)}, f32[256]{0:T(256)}) conditional(s32[]{:T(128)} %convert_element_type.7, (s32[5]{0:T(128)S(1)}, s32[1,256]{1,0:T(1,128)S(1)}, f32[1,256]{1,0:T(1,128)S(1)}, bf16[256,256]{1,0:T(8,128)(2,1)S(1)}, f32[96,512]{1,0:T(8,128)S(1)}, /*index=5*/f32[96,512]{1,0:T(8,128)S(1)}, f32[96,256]{1,0:T(8,128)}, ...), branch_computations={%region_2.3_spmd, %region_3.6_spmd} | conditional | flops 98307 | bytes 19690360 | solution.py:364
  43.4 2.5 %finish.2 = (bf16[256,256]{1,0:T(8,128)(2,1)}, f32[1,256]{1,0:T(1,128)}) custom-call(s32[5]{0:T(128)S(1)} %get-tuple-element.263.place_ref, s32[1,256]{1,0:T(1,128)S(1)} %get-tuple-element.264.pivots_ref, f32[1,256]{1,0:T(1,128)S(1)} %get-tuple-element.265.diag_ref, bf16[256,256]{1,0:T(8,128)(2,1)S(1)} %get-tuple-element.266.previous_ref, ...), custom_call_target="tpu_custom_call" | custom-call | tf_op jit(solution)/shard_map/cond/branch_0_fun/finish/pallas_call | solution.py:213
  (30 shorter events, 1.4 us)
Async XLA Ops:
  0.6 8.8 %copy-start = (bf16[768,1024]{1,0:T(8,128)(2,1)S(1)}, bf16[768,1024]{1,0:T(8,128)(2,1)}, u32[]{:S(2)}) copy-start(bf16[768,1024]{1,0:T(8,128)(2,1)} %refs_2_.1) | copy-start | bytes 4718596
  0.7 10.7 %copy-start.20 = (s32[16,4]{0,1:T(4,128)S(1)}, s32[16,4]{0,1:T(4,128)}, u32[]{:S(2)}) copy-start(s32[16,4]{0,1:T(4,128)} %param.21) | copy-start | bytes 772
  3.8 10.5 %collective-permute-start.11 = (bf16[96,768]{1,0:T(8,128)(2,1)}, bf16[96,768]{1,0:T(8,128)(2,1)S(1)}, u32[]{:S(2)}, u32[]{:S(2)}) collective-permute-start(bf16[96,768]{1,0:T(8,128)(2,1)} %select.15.refs_0_), channel_id=1, source_target_pairs={{0,12},{4,8},{8,4},{12,0},{1,13},{5,9},{9,5},{13,1},{2,14},{6,10},... | collective-permute-start | bytes 442376 | tf_op jit(solution)/shard_map/ppermute | solution.py:253
  8.8 12.7 %collective-permute-start.10 = (bf16[96,768]{1,0:T(8,128)(2,1)}, bf16[96,768]{1,0:T(8,128)(2,1)S(1)}, u32[]{:S(2)}, u32[]{:S(2)}) collective-permute-start(bf16[96,768]{1,0:T(8,128)(2,1)} %select.15.refs_0_), channel_id=1, source_target_pairs={{0,8},{4,12},{8,0},{12,4},{1,9},{5,13},{9,1},{13,5},{2,10},{6,14},... | collective-permute-start | bytes 442376 | tf_op jit(solution)/shard_map/ppermute | solution.py:253
  8.8 15.6 %collective-permute-start.7 = (bf16[96,768]{1,0:T(8,128)(2,1)}, bf16[96,768]{1,0:T(8,128)(2,1)S(1)}, u32[]{:S(2)}, u32[]{:S(2)}) collective-permute-start(bf16[96,768]{1,0:T(8,128)(2,1)} %select.15.refs_0_), channel_id=1, source_target_pairs={{0,4},{4,0},{8,12},{12,8},{1,5},{5,1},{9,13},{13,9},{2,6},{6,2},{1... | collective-permute-start | bytes 442376 | tf_op jit(solution)/shard_map/ppermute | solution.py:253
  11.5 13.0 %copy-start.13 = (s32[256]{0:T(256)S(1)}, s32[256]{0:T(256)}, u32[]{:S(2)}) copy-start(s32[256]{0:T(256)} %param.17) | copy-start | bytes 3076
  11.5 20.0 %collective-permute-start.5 = (f32[96,512]{1,0:T(8,128)}, f32[96,512]{1,0:T(8,128)S(1)}, u32[]{:S(2)}, u32[]{:S(2)}) collective-permute-start(f32[96,512]{1,0:T(8,128)} %get-tuple-element.321), channel_id=1, source_target_pairs={{0,1},{1,0},{2,3},{3,2},{4,5},{5,4},{6,7},{7,6},{8,9},{9,8},{10,11... | collective-permute-start | bytes 589832 | tf_op jit(solution)/shard_map/ppermute | solution.py:253
  14.3 7.3 %copy-start.15 = (bf16[96,768]{1,0:T(8,128)(2,1)}, bf16[96,768]{1,0:T(8,128)(2,1)S(1)}, u32[]{:S(2)}) copy-start(bf16[96,768]{1,0:T(8,128)(2,1)S(1)} %collective-permute-done.11.refs_1_) | copy-start | bytes 442372
  21.5 0.7 %copy-start.16 = (bf16[96,768]{1,0:T(8,128)(2,1)}, bf16[96,768]{1,0:T(8,128)(2,1)S(1)}, u32[]{:S(2)}) copy-start(bf16[96,768]{1,0:T(8,128)(2,1)S(1)} %collective-permute-done.10.refs_0_) | copy-start | bytes 442372
  24.4 9.2 %collective-permute-start.12 = (f32[192,512]{1,0:T(8,128)}, f32[192,512]{1,0:T(8,128)S(1)}, u32[]{:S(2)}, u32[]{:S(2)}) collective-permute-start(f32[192,512]{1,0:T(8,128)} %get-tuple-element.325), channel_id=1, source_target_pairs={{0,1},{1,0},{2,3},{3,2},{4,5},{5,4},{6,7},{7,6},{8,9},{9,8},{10,11... | collective-permute-start | bytes 1179656 | tf_op jit(solution)/shard_map/ppermute | solution.py:253
  24.5 18.9 %copy-start.12 = (bf16[256,256]{1,0:T(8,128)(2,1)S(1)}, bf16[256,256]{1,0:T(8,128)(2,1)}, u32[]{:S(2)}) copy-start(bf16[256,256]{1,0:T(8,128)(2,1)} %param.16) | copy-start | bytes 393220
  24.5 18.9 %copy-start.17 = (f32[256]{0:T(256)S(1)}, f32[256]{0:T(256)}, u32[]{:S(2)}) copy-start(f32[256]{0:T(256)} %param.18) | copy-start | bytes 3076
  24.5 0.7 %copy-start.14 = (bf16[96,768]{1,0:T(8,128)(2,1)}, bf16[96,768]{1,0:T(8,128)(2,1)S(1)}, u32[]{:S(2)}) copy-start(bf16[96,768]{1,0:T(8,128)(2,1)S(1)} %collective-permute-done.7.refs_0_) | copy-start | bytes 442372
  27.2 7.7 %collective-permute-start.8 = (f32[96,512]{1,0:T(8,128)}, f32[96,512]{1,0:T(8,128)S(1)}, u32[]{:S(2)}, u32[]{:S(2)}) collective-permute-start(f32[96,512]{1,0:T(8,128)} %get-tuple-element.323), channel_id=1, source_target_pairs={{0,1},{1,0},{2,3},{3,2},{4,5},{5,4},{6,7},{7,6},{8,9},{9,8},{10,11... | collective-permute-start | bytes 589832 | tf_op jit(solution)/shard_map/ppermute | solution.py:253
  27.7 12.9 %all-to-all-start = ((bf16[4,128,256]{2,1,0:T(8,128)(2,1)}), bf16[4,128,256]{2,1,0:T(8,128)(2,1)S(1)}, u32[]{:S(2)}, u32[]{:S(2)}) async-start(bf16[4,128,256]{2,1,0:T(8,128)(2,1)} %ket.1), calls=%async_computation | async-start | bytes 524288 | tf_op jit(solution)/shard_map/all_to_all | solution.py:329
  32.1 11.0 %collective-permute-start.6 = (f32[96,256]{1,0:T(8,128)}, f32[96,256]{1,0:T(8,128)}, u32[]{:S(2)}, u32[]{:S(2)}) collective-permute-start(f32[96,256]{1,0:T(8,128)} %slice_add_fusion.3), channel_id=1, source_target_pairs={{0,2},{2,0},{1,3},{3,1},{4,6},{6,4},{5,7},{7,5},{8,10},{10,8},{9,1... | collective-permute-start | bytes 294920 | tf_op jit(solution)/shard_map/ppermute | solution.py:253
  34.3 9.0 %collective-permute-start.13 = (f32[192,256]{1,0:T(8,128)}, f32[192,256]{1,0:T(8,128)}, u32[]{:S(2)}, u32[]{:S(2)}) collective-permute-start(f32[192,256]{1,0:T(8,128)} %slice_add_fusion.1), channel_id=1, source_target_pairs={{0,2},{2,0},{1,3},{3,1},{4,6},{6,4},{5,7},{7,5},{8,10},{10,8},{9,1... | collective-permute-start | bytes 589832 | tf_op jit(solution)/shard_map/ppermute | solution.py:253
  35.5 7.8 %collective-permute-start.9 = (f32[96,256]{1,0:T(8,128)}, f32[96,256]{1,0:T(8,128)}, u32[]{:S(2)}, u32[]{:S(2)}) collective-permute-start(f32[96,256]{1,0:T(8,128)} %slice_add_fusion.2), channel_id=1, source_target_pairs={{0,2},{2,0},{1,3},{3,1},{4,6},{6,4},{5,7},{7,5},{8,10},{10,8},{9,1... | collective-permute-start | bytes 294920 | tf_op jit(solution)/shard_map/ppermute | solution.py:253
  40.5 0.7 %copy-start.11 = (bf16[4,128,256]{2,1,0:T(8,128)(2,1)}, bf16[4,128,256]{2,1,0:T(8,128)(2,1)S(1)}, u32[]{:S(2)}) copy-start(bf16[4,128,256]{2,1,0:T(8,128)(2,1)S(1)} %all-to-all-done.incoming_ref) | copy-start | bytes 786436
